TPU v7x, 32 devices: a whole 2x2x4 slice. The times are simulated.
32 devices in a mesh: gx: 4 (over y, core), yz: 8 (over z, x).
Axes of the slice: x: 2, y: 2, z: 4, core: 2. Of those that a mesh axis runs over, the one named last changes fastest.
Arguments:
- orbitals: bfloat16 [4, 8, 9, 128, 256], P('gx', 'yz'), may hold values from -0.125 to 0.125
- potential: float32 [4, 8, 256], P('gx', 'yz'), may hold values from 0.25 to 4
- density: bfloat16 [4, 8, 9, 128, 128], P('gx', 'yz'), may hold values from -0.1 to 0.6
- pattern: int32 [4, 8, 9], P('gx', 'yz'), may hold values 0 or 1
Outputs:
- hamiltonian: float32 [4, 8, 9, 128, 128], P('gx', 'yz')
- margin: float32 [4, 8, 9, 128, 128], P('gx', 'yz')
- purified: float32 [4, 8, 9, 128, 128], P('gx', 'yz')
All inputs are finite; a program needn't handle non-finite values. No bound on the sum of `pattern` on one device may be relied on, other than what follows from the above.
Results may differ from a plain program's by a relative error of at most 0.0068.
Values may be sent and summed in bfloat16 or wider, within the bound.
A program may use at most 64 MiB of HBM per device.

v0:
```python
import functools

import jax
import jax.numpy as jnp
from jax import lax
from jax.experimental import pallas as pl
from jax.experimental.pallas import tpu as pltpu
from jax.sharding import PartitionSpec as P

MESH = pl.DeviceIdType.MESH
SPAN = (-1, 0, 1)


def part(d):
    return pl.ds(1, 2) if d == 1 else pl.ds(0, 2) if d == -1 else pl.ds(0, 3)


class Halo:
    def __init__(self, where, own, near, send, recv, sign=1, whole=False, slim=False):
        self.where, self.own, self.near = where, own, near
        self.send, self.recv, self.sign, self.whole, self.slim = send, recv, sign, whole, slim
        outer = 2 * lax.rem(lax.axis_index("gx"), 2) - 1
        self.order = [
            (db, piece, pa, das)
            for piece, pa, das in (
                ((0, None, (1, -1)),) if whole else
                ((0, 1, (1, -1)), (1, 0, ()), (2, 2, ())) if slim else (
                    (0, 1, (outer, -outer)),
                    (1, 1 + sign * outer, (outer,)),
                    (2, 1 - sign * outer, (-outer,)),
                )
            )
            for db in (1, -1)
        ]
        self.direct = {}
        self.passed = []
        self.next = 0

    def make(self, src, da, db, ta, tb, pa, pb=None):
        dst = self.near.at[1 - da, 1 - db]
        if not self.whole:
            pb = part(self.sign * db) if pb is None else pb
            src = src.at[pa, pb]
            dst = dst.at[pa, pb]
        at = self.next
        self.next += 1
        copy = pltpu.make_async_remote_copy(
            src_ref=src, dst_ref=dst, send_sem=self.send.at[at], recv_sem=self.recv.at[at],
            device_id=self.where(ta, tb), device_id_type=MESH,
        )
        copy.start()
        return copy

    def start_far(self):
        for db, piece, pa, _ in self.order:
            self.direct[db, piece] = self.make(self.own, 0, db, 0, db, pa)

    def start_near(self):
        for da in (1, -1):
            pa = 1 if self.slim else part(self.sign * da)
            self.direct[da] = self.make(self.own, da, 0, da, 0, pa)

    def start(self):
        self.start_far()
        self.start_near()

    def relay(self):
        for db, piece, pa, das in self.order:
            if das:
                self.direct[db, piece].wait_recv()
            for da in das:
                src = self.near.at[1, 1 - db]
                pb = 1 if self.slim else None
                self.passed.append(self.make(src, da, db, da, 0, pa, pb))

    def finish(self):
        for db, piece, _, das in self.order:
            if not das:
                self.direct[db, piece].wait_recv()
        for da in (1, -1):
            self.direct[da].wait_recv()
        for copy in self.passed:
            copy.wait_recv()

    def drain(self):
        for copy in list(self.direct.values()) + self.passed:
            copy.wait_send()


def product(left, own, near, keep, emit):
    width = left.shape[-1]
    blank = jnp.zeros((width, width), jnp.bfloat16)
    for pa in SPAN:
        total = None
        for fa in SPAN:
            if abs(pa - fa) > 1:
                continue
            lhs = jnp.concatenate([left[fa + 1, fb + 1] for fb in SPAN], axis=1)
            rows = []
            for fb in SPAN:
                src = own if (fa, fb) == (0, 0) else near.at[fa + 1, fb + 1]
                rows.append(jnp.concatenate(
                    [src[pa - fa + 1, pb - fb + 1] if abs(pb - fb) <= 1 else blank for pb in SPAN],
                    axis=1,
                ))
            rhs = jnp.concatenate(rows, axis=0)
            term = jnp.dot(lhs, rhs, preferred_element_type=jnp.float32)
            total = term if total is None else total + term
        for pb in SPAN:
            cut = total[:, (pb + 1) * width:(pb + 2) * width]
            emit(pa + 1, pb + 1, cut * keep[pa + 1, pb + 1])


def overlap(lefts, rights, width, emit):
    for pa in SPAN:
        total = None
        for ka in SPAN:
            if abs(ka - pa) > 1:
                continue
            for kb in SPAN:
                lhs = lefts(ka, kb)
                rhs = rights(ka, kb)
                blank = jnp.zeros(lhs.shape, jnp.bfloat16)
                rows = jnp.concatenate(
                    [rhs[ka - pa + 1, kb - pb + 1] if abs(kb - pb) <= 1 else blank for pb in SPAN],
                    axis=0,
                )
                term = lax.dot_general(
                    lhs, rows, (((1,), (1,)), ((), ())), preferred_element_type=jnp.float32
                )
                total = term if total is None else total + term
        for pb in SPAN:
            cut = total[:, (pb + 1) * width:(pb + 2) * width]
            emit(pa + 1, pb + 1, cut)


def kernel(counts, orb, pot, den, pattern, ham, mar, pur,
           o_near, v_near, w_near, d0_near, d1_near, m_near, u_near, t0_near, t1_near, first, send, recv):
    width, cells = orb.shape[-2], orb.shape[-1]
    me = (lax.axis_index("gx"), lax.axis_index("yz"))

    def where(da, db):
        return (
            lax.rem(me[0] + da + counts[0], counts[0]),
            lax.rem(me[1] + db + counts[1], counts[1]),
        )

    keep = {
        (a, b): pattern[3 * a + b].astype(jnp.float32) for a in range(3) for b in range(3)
    }
    barrier = pltpu.get_barrier_semaphore()
    for da, db in ((0, 1), (0, -1), (1, 0), (-1, 0)):
        pl.semaphore_signal(barrier, inc=1, device_id=where(da, db), device_id_type=MESH)
    pl.semaphore_wait(barrier, 4)

    used = iter(range(7))

    def halo(own, near, **more):
        at = next(used)
        return Halo(where, own, near, send.at[at], recv.at[at], **more)

    waves = halo(orb, o_near, sign=-1)
    v_own = v_near.at[1, 1]
    v_own[0:1] = pot[0]
    for a in range(3):
        for b in range(3):
            at = 1 + 3 * a + b
            v_own[at:at + 1] = jnp.full((1, cells), keep[a, b], jnp.float32)
    fields = halo(v_own, v_near, whole=True)
    fields.start()
    waves.start()
    d_own = d0_near.at[1, 1]
    for a in range(3):
        for b in range(3):
            d_own[a, b] = (den[a, b].astype(jnp.float32) * keep[a, b]).astype(jnp.bfloat16)
    density = halo(d_own, d0_near)
    density.start_far()
    def region(ka, kb):
        return orb if (ka, kb) == (0, 0) else o_near.at[ka + 1, kb + 1]

    def prepare(regions):
        lane = lax.broadcasted_iota(jnp.int32, (width, 128), 1)
        for ka, kb in regions:
            src = region(ka, kb)
            field = pot[0] if (ka, kb) == (0, 0) else v_near[ka + 1, kb + 1, 0:1]
            for la in SPAN:
                for lb in SPAN:
                    if abs(ka - la) > 1 or abs(kb - lb) > 1:
                        continue
                    value = src[la + 1, lb + 1].astype(jnp.float32)
                    dst = w_near.at[ka + 1, kb + 1, la + 1, lb + 1]
                    dst[:, :cells] = (value * field).astype(jnp.bfloat16)
                    for line in range(cells // 128):
                        piece = value[:, line * 128:(line + 1) * 128]
                        ahead = pltpu.roll(piece, 127, 1)
                        step = jnp.where(lane < 127, ahead - piece, 0.0)
                        at = cells + line * 128
                        dst[:, at:at + 128] = step.astype(jnp.bfloat16)

    fields.relay()
    prepare([(0, 0)])
    waves.relay()
    density.start_near()
    prepare([(0, 1), (0, -1)])
    waves.finish()

    m_own, u_own = m_near.at[1, 1], u_near.at[1, 1]

    def put_margin(a, b, value):
        kept = value * keep[a, b]
        mar[a, b] = kept
        m_own[a, b] = kept.astype(jnp.bfloat16)
        u_own[a, b] = value.astype(jnp.bfloat16)

    overlap(lambda ka, kb: region(ka, kb)[ka + 1, kb + 1], region, width, put_margin)
    margin = halo(u_own, u_near, slim=True)
    margin.start()
    fields.finish()
    density.relay()
    margin.relay()

    def h_left(ka, kb):
        half = w_near[ka + 1, kb + 1, ka + 1, kb + 1][:, cells:] * 0.5
        return jnp.concatenate([region(ka, kb)[ka + 1, kb + 1], half.astype(jnp.bfloat16)], axis=1)

    def put_ham(a, b, value):
        ham[a, b] = value * keep[a, b]

    def complete(local):
        for ja in SPAN:
            for jb in SPAN:
                for ka in SPAN:
                    for kb in SPAN:
                        pa, pb = ka - ja, kb - jb
                        if (ja, jb) == (0, 0) or abs(pa) > 1 or abs(pb) > 1:
                            continue
                        if local != ((ka, kb) == (0, 0)):
                            continue
                        sent = (pa, pb) == (0, 0) or ja == 0 or (jb == 0 and pa == 0)
                        if sent and not local:
                            block = u_near[ja + 1, jb + 1, pa + 1, pb + 1].astype(jnp.float32)
                        else:
                            block = u_near[ka + 1, kb + 1, 1 - pa, 1 - pb].astype(jnp.float32).T
                        at = 1 + 3 * (pa + 1) + pb + 1
                        kept = block * v_near[ja + 1, jb + 1, at:at + 1, :width]
                        m_near[ja + 1, jb + 1, pa + 1, pb + 1] = kept.astype(jnp.bfloat16)

    complete(True)
    margin.finish()
    complete(False)
    density.finish()

    def put_first(a, b, value):
        first[a, b] = value.astype(jnp.bfloat16)

    started = [waves, fields, density, margin]
    nears = ((d0_near, t0_near), (d1_near, t1_near))
    for turn, (d_near, t_near) in enumerate(nears):
        d_row, t_row = d_near.at[1, 1], t_near.at[1, 1]
        product(d_row, m_own, m_near, keep, put_first)
        if turn:
            rows.relay()
            overlap(h_left, lambda ka, kb: w_near.at[ka + 1, kb + 1], width, put_ham)
            rows.finish()

        def put_third(a, b, value):
            pur[a, b] = 3.0 * value
            t_row[a, b] = value.astype(jnp.bfloat16)

        product(first, d_row, d_near, keep, put_third)
        cubic = halo(t_row, t_near)
        cubic.start()
        cubic.relay()
        if not turn:
            prepare([(ka, kb) for ka in (-1, 1) for kb in SPAN])
        cubic.finish()
        started.append(cubic)
        after = nears[turn + 1][0].at[1, 1] if turn + 1 < len(nears) else None

        def put_fifth(a, b, value):
            result = pur[a, b] - 2.0 * value
            pur[a, b] = result
            if after is not None:
                after[a, b] = result.astype(jnp.bfloat16)

        product(first, t_row, t_near, keep, put_fifth)
        if after is not None:
            rows = halo(after, nears[turn + 1][0])
            rows.start()
            started.append(rows)
    for one in started:
        one.drain()


def body(counts, orbitals, potential, density, pattern):
    width, cells = orbitals.shape[3], orbitals.shape[4]
    near = pltpu.VMEM((3, 3, 3, 3, width, width), jnp.bfloat16)
    blocks = jax.ShapeDtypeStruct((3, 3, width, width), jnp.float32)
    vmem = pl.BlockSpec(memory_space=pltpu.VMEM)
    outs = pl.pallas_call(
        functools.partial(kernel, counts),
        out_shape=(blocks,) * 3,
        in_specs=[vmem, vmem, vmem, pl.BlockSpec(memory_space=pltpu.SMEM)],
        out_specs=(vmem,) * 3,
        scratch_shapes=[
            pltpu.VMEM((3, 3, 3, 3, width, cells), jnp.bfloat16),
            pltpu.VMEM((3, 3, 16, cells), jnp.float32),
            pltpu.VMEM((3, 3, 3, 3, width, 2 * cells), jnp.bfloat16),
            near, near, near, near, near, near,
            pltpu.VMEM((3, 3, width, width), jnp.bfloat16),
            pltpu.SemaphoreType.DMA((7, 16)),
            pltpu.SemaphoreType.DMA((7, 16)),
        ],
        compiler_params=pltpu.CompilerParams(
            collective_id=0, has_side_effects=True, vmem_limit_bytes=44 * 2**20
        ),
    )(
        orbitals.reshape(3, 3, width, cells),
        potential.reshape(1, 1, cells),
        density.reshape(3, 3, width, width),
        pattern.reshape(9),
    )
    return tuple(out.reshape(1, 1, 9, width, width) for out in outs)


def solution(mesh):
    rows = P("gx", "yz", None, None, None)
    flat = P("gx", "yz", None)
    return jax.shard_map(
        functools.partial(body, (mesh.shape["gx"], mesh.shape["yz"])),
        mesh=mesh,
        in_specs=(rows, flat, rows, flat),
        out_specs=(rows,) * 3,
        check_vma=False,
    )
```

profile of v0, /device:TPU:1, one launch (start us, length us, event | category | flops | bytes accessed | tf_op | source)
XLA Modules:
  0.0 99.5 jit_solution(11707601933339187584)
XLA Ops:
  0.6 0.0 copy-start.2
  0.6 0.0 copy-start.3
  0.7 0.7 copy-done.2
  1.3 0.0 copy-done.3
  1.3 0.0 copy-start
  1.3 1.1 %copy-done = bf16[1,1,9,128,256]{4,3,2,1,0:T(8,128)(2,1)S(1)} copy-done((bf16[1,1,9,128,256]{4,3,2,1,0:T(8,128)(2,1)S(1)}, bf16[1,1,9,128,256]{4,3,2,1,0:T(8,128)(2,1)}, u32[]{:S(2)}) %copy-start) | copy-done | bytes 589848
  2.4 0.0 copy-start.1
  2.4 1.0 copy-done.1
  3.3 93.7 %shard_map.67 = (f32[3,3,128,128]{3,2,1,0:T(8,128)S(1)}, f32[3,3,128,128]{3,2,1,0:T(8,128)S(1)}, f32[3,3,128,128]{3,2,1,0:T(8,128)S(1)}) custom-call(bf16[3,3,128,256]{3,2,1,0:T(8,128)(2,1)S(1)} %bitcast.9, f32[1,1,256]{2,1,0:T(1,128)S(1)} %copy-done.2, bf16[3,3,128,128]{3,2,1,0:T(8,128)(2,1)S(1)} %bitcast.10, s32[9]{0:T(128)S(1)} %bitcast.11), custom_call_target="tpu_custom_call" | custom-call | tf_op jit(solution)/shard_map/pallas_call | solution.py:300
  97.0 0.8 copy.10
  97.9 0.8 copy.11
  98.7 0.8 copy.12
Async XLA Ops:
  0.6 0.7 copy-start.2
  0.6 0.7 copy-start.3
  1.3 1.1 %copy-start = (bf16[1,1,9,128,256]{4,3,2,1,0:T(8,128)(2,1)S(1)}, bf16[1,1,9,128,256]{4,3,2,1,0:T(8,128)(2,1)}, u32[]{:S(2)}) copy-start(bf16[1,1,9,128,256]{4,3,2,1,0:T(8,128)(2,1)} %param.4) | copy-start | bytes 1769476
  2.4 1.0 copy-start.1
where the time goes:
time: 99.7 us; the launch traced here: 99.5 us
  Pallas kernels  93.7 us (94%)
  local copies, waits for them, and re-layouts  5.14 us (5%)
    pallas_call x1, Pallas kernels, body(): pl.pallas_call(functools.partial(kernel, counts), out_shape=(blocks,) * 3...  93.7 us
    unnamed x11, local copies, waits for them, and re-layouts  5.14 us

commit v1 on v0

v1 whole, which is shorter than its diff:
```python
import functools

import jax
import jax.numpy as jnp
from jax import lax
from jax.experimental import pallas as pl
from jax.experimental.pallas import tpu as pltpu
from jax.sharding import PartitionSpec as P

MESH = pl.DeviceIdType.MESH
SPAN = (-1, 0, 1)
AROUND = [(a, b) for a in SPAN for b in SPAN if (a, b) != (0, 0)]
PORTS = 144


def part(d):
    return pl.ds(1, 2) if d == 1 else pl.ds(0, 2) if d == -1 else pl.ds(0, 3)


class Either:
    def __init__(self, copy, apart):
        self.copy, self.apart = copy, apart

    def wait_recv(self):
        pl.when(self.apart)(lambda: self.copy.wait_recv())

    def wait_send(self):
        pl.when(self.apart)(lambda: self.copy.wait_send())


class Wire:
    def __init__(self, send, recv):
        self.send, self.recv = send, recv
        self.ports = iter(range(PORTS))
        self.started = []

    def __call__(self, src, dst, device, apart=None):
        at = next(self.ports)
        copy = pltpu.make_async_remote_copy(
            src_ref=src, dst_ref=dst, send_sem=self.send.at[at], recv_sem=self.recv.at[at],
            device_id=device, device_id_type=MESH,
        )
        if apart is None:
            copy.start()
        else:
            pl.when(apart)(lambda: copy.start())

            @pl.when(jnp.logical_not(apart))
            def _():
                dst[...] = src[...]

            copy = Either(copy, apart)
        self.started.append(copy)
        return copy

    def drain(self):
        for copy in self.started:
            copy.wait_send()


class Places:
    def __init__(self, counts):
        self.counts = counts
        many = counts[1]
        self.table = list(range(many))
        if many % 2 == 0 and many >= 8:
            tall = many // 2
            self.table = [2, 0] + [2 * z + 1 for z in range(tall)] + [2 * z for z in range(tall - 1, 1, -1)]
        self.roles = [self.table.index(b) for b in range(many)]
        self.a, self.b = lax.axis_index("gx"), lax.axis_index("yz")
        self.c = self.pick(self.roles, self.b)
        self.outer = 2 * lax.rem(self.a, 2) - 1

    def pick(self, table, at):
        value = jnp.int32(table[0])
        for i in range(1, len(table)):
            value = jnp.where(at == i, jnp.int32(table[i]), value)
        return value

    def row(self, da):
        return lax.rem(self.a + da + self.counts[0], self.counts[0])

    def ring(self, b):
        return lax.rem(b + self.counts[1], self.counts[1])

    def seat(self, b):
        return self.pick(self.table, self.ring(b))

    def home(self, da, db):
        return self.row(da), self.ring(self.b + db)

    def near(self, da, db):
        return self.row(da), self.seat(self.c + db)

    def inward(self, db):
        return self.a, self.seat(self.b + db)

    def apart(self, db):
        return self.ring(self.b + db) != self.c

    def outward(self, da, db):
        return self.row(da), self.ring(self.c + db)

    def away(self, db):
        return self.ring(self.c + db) != self.b

    def greet(self, barrier):
        many = self.counts[1]
        lists = []
        for b in range(many):
            c, met = self.roles[b], set()
            for db in SPAN:
                met |= {(b + db) % many, self.table[(b + db) % many]}
                met |= {(c + db) % many, self.table[(c + db) % many]}
            lists.append(sorted(met - {b}))
        for at in range(max(len(met) for met in lists)):
            to = self.pick([met[at] if at < len(met) else -1 for met in lists], self.b)

            @pl.when(to >= 0)
            def _():
                for da in SPAN:
                    pl.semaphore_signal(
                        barrier, inc=1, device_id=(self.row(da), to), device_id_type=MESH
                    )

        for da in (1, -1):
            pl.semaphore_signal(barrier, inc=1, device_id=(self.row(da), self.b), device_id_type=MESH)
        return self.pick([3 * len(met) + 2 for met in lists], self.b)


class Halo:
    def __init__(self, wire, places, near, base=None, whole=False, split=False):
        self.wire, self.places, self.near, self.base = wire, places, near, base
        self.whole, self.split = whole, split
        outer = places.outer
        self.order = [
            (db, piece, pa, das)
            for piece, pa, das in (
                ((0, None, (1, -1)),) if whole else (
                    (0, 1, (outer, -outer)),
                    (2, 1 - outer, (-outer,)),
                    (1, 1 + outer, () if split else (outer,)),
                )
            )
            for db in ((1, -1) if base is None else (0, 1, -1))
        ]
        self.direct = {}
        self.passed = []

    def make(self, src, da, db, device, pa, apart=None):
        dst = self.near.at[1 - da, 1 - db]
        if not self.whole:
            src = src.at[pa, part(db)]
            dst = dst.at[pa, part(db)]
        return self.wire(src, dst, device, apart)

    def start_far(self, which=None):
        for db, piece, pa, _ in self.order:
            if which is not None and piece != which:
                continue
            if self.base is None:
                copy = self.make(self.near.at[1, 1], 0, db, self.places.near(0, db), pa)
            else:
                copy = self.make(self.base, 0, db, self.places.inward(db), pa, self.places.apart(db))
            self.direct[db, piece] = copy

    def start_near(self, name):
        outer = self.places.outer
        da, pa = {
            "turned": (outer, 1 + outer), "outer": (outer, 1),
            "inner": (-outer, 1), "last": (-outer, 1 - outer),
        }[name]
        self.direct[name] = self.make(self.near.at[1, 1], da, 0, self.places.near(da, 0), pa)

    def ready(self, at):
        if at == 0:
            self.start_near("turned")
        elif at == 1:
            self.start_far(0)
            self.start_near("outer")
            self.start_near("inner")
        else:
            self.start_far(2)
            self.start_far(1)
            self.start_near("last")

    def relay(self, start=0, stop=None):
        for db, piece, pa, das in self.order[start:stop]:
            if das:
                self.direct[db, piece].wait_recv()
            for at, da in enumerate(das):
                src = self.near.at[1, 1 - db]
                copy = self.make(src, da, db, self.places.near(da, 0), pa)
                self.passed.append((piece == 2 or at == 1, copy))

    def cross(self):
        outer = self.places.outer
        self.direct["turned"].wait_recv()
        for db in (1, -1):
            src = self.near.at[1 + outer, 1, 1 - outer, part(db)]
            dst = self.near.at[1 + outer, 1 - db, 1 - outer, part(db)]
            self.passed.append((False, self.wire(src, dst, self.places.near(0, db))))

    def finish_inner(self):
        for db, piece, _, das in self.order:
            if not das:
                self.direct[db, piece].wait_recv()
        for name in ("inner", "last"):
            self.direct[name].wait_recv()
        for inner, copy in self.passed:
            if inner:
                copy.wait_recv()

    def finish_outer(self):
        self.direct["outer"].wait_recv()
        for inner, copy in self.passed:
            if not inner:
                copy.wait_recv()

    def finish(self):
        for _, copy in self.passed:
            copy.wait_recv()


class Slim:
    def __init__(self, wire, places, near):
        self.wire, self.places, self.near = wire, places, near
        self.far, self.close, self.passed = {}, [], []

    def start_far(self):
        own = self.near.at[1, 1]
        for db in (1, -1):
            dst = self.near.at[1, 1 - db]
            self.far[db] = self.wire(
                own.at[pl.ds(0, 3), 1], dst.at[pl.ds(0, 3), 1], self.places.near(0, db)
            )

    def start_near(self):
        own = self.near.at[1, 1]
        for da in (1, -1):
            dst = self.near.at[1 - da, 1]
            to = self.places.near(da, 0)
            self.close.append(self.wire(own.at[1], dst.at[1], to))
            for pb in (0, 2):
                self.close.append(self.wire(own.at[1 + da, pb], dst.at[1 + da, pb], to))

    def relay(self):
        for db in (1, -1):
            self.far[db].wait_recv()
            for da in (1, -1):
                src = self.near.at[1, 1 - db, 1, 1]
                dst = self.near.at[1 - da, 1 - db, 1, 1]
                self.passed.append(self.wire(src, dst, self.places.near(da, 0)))

    def finish(self):
        for copy in self.close + self.passed:
            copy.wait_recv()

    @staticmethod
    def sent(ja, jb, pa, pb):
        if (pa, pb) == (0, 0):
            return True
        if ja == 0:
            return pb == 0
        return jb == 0 and pb != 0 and pa in (0, -ja)


def groups(outer):
    return ((outer, (0, outer)), (0, (0, outer, -outer)), (-outer, (0, -outer)))


def product(left, near, outer, emit, done):
    width = left.shape[-1]
    blank = jnp.zeros((width, width), jnp.bfloat16)
    for at, (pa, fas) in enumerate(groups(outer)):
        total = None
        for fa in fas:
            lhs = jnp.concatenate([left[fa + 1, fb + 1] for fb in SPAN], axis=1)
            rhs = jnp.concatenate([
                jnp.concatenate([
                    near[fa + 1, fb + 1, pa - fa + 1, pb - fb + 1] if abs(pb - fb) <= 1 else blank
                    for pb in SPAN
                ], axis=1) for fb in SPAN
            ], axis=0)
            term = jnp.dot(lhs, rhs, preferred_element_type=jnp.float32)
            total = term if total is None else total + term
        for pb in SPAN:
            emit(pa, pb, total[:, (pb + 1) * width:(pb + 2) * width])
        done(at)


def column(width, lefts, rights, turned, ka, fas, base=None):
    blank = jnp.zeros((width, width), jnp.bfloat16)
    inner = [(fa, fb) for fa in fas for fb in SPAN]
    lhs = jnp.concatenate([
        jnp.concatenate(
            [lefts((ka, kb), f) if abs(f[1] - kb) <= 1 else blank for f in inner], axis=1
        ) for kb in SPAN
    ], axis=0)
    rhs = jnp.concatenate([rights(f) for f in inner], axis=1 if turned else 0)
    total = lax.dot_general(
        lhs, rhs, (((1,), (1 if turned else 0,)), ((), ())), preferred_element_type=jnp.float32
    )
    return total if base is None else total + base


def give(width, ka, total, emit):
    for kb in SPAN:
        emit(ka, kb, total[(kb + 1) * width:(kb + 2) * width])


class Gram:
    A_PAIRS = ((0, 1, 1), (1, 1, 0), (4, -1, -1), (5, 0, -1), (8, 0, 0))
    B_PAIRS = ((2, 1, 1), (3, 1, 0), (6, -1, -1), (7, -1, 0), (9, 0, -1), (10, 0, 0), (11, 0, 1))
    MIDDLE = ((0, 8), (0, 5), (0, 1), (1, 9), (1, 10), (1, 11), (2, 9), (2, 10), (2, 11))
    CHUNKS = (pl.ds(0, 4), pl.ds(4, 4), pl.ds(8, 4))

    def __init__(self, wire, places, lefts, rights, own, out, into, out_far, into_far, out_mid=None, into_mid=None):
        self.wire, self.places, self.outer = wire, places, places.outer
        self.lefts, self.rights = lefts, rights
        self.own, self.out, self.into, self.out_far, self.into_far = own, out, into, out_far, into_far
        self.out_mid, self.into_mid = out_mid, into_mid
        self.width = lefts.shape[2]
        self.first = {}
        self.second = {}

    def dot(self, ka, la):
        tall = 3 * self.width
        lhs = self.lefts[1 + ka].reshape(tall, self.lefts.shape[3])
        rhs = self.rights[1 + la].reshape(tall, self.rights.shape[3])
        return lax.dot_general(lhs, rhs, (((1,), (1,)), ((), ())), preferred_element_type=jnp.float32)

    def cut(self, value, kb, lb):
        w = self.width
        return value[(kb + 1) * w:(kb + 2) * w, (lb + 1) * w:(lb + 2) * w]

    def compute_sent(self, side):
        ka = self.outer if side else -self.outer
        for la, pairs in ((ka, self.A_PAIRS), (0, self.B_PAIRS)):
            value = self.dot(ka, la)
            for at, kb, lb in pairs:
                self.out[side, at] = self.cut(value, kb, lb).astype(jnp.bfloat16)

    def start(self, side, chunk):
        da = -self.outer if side else self.outer
        at = self.CHUNKS[chunk]
        self.first[side, chunk] = self.wire(self.out.at[side, at], self.into.at[side, at], self.places.home(da, 0))

    def compute_own(self):
        for q, la in enumerate((0, -self.outer, self.outer)):
            value = self.dot(0, la)
            for at, kb, lb in (self.B_PAIRS if q else self.A_PAIRS):
                self.own[q, at] = self.cut(value, kb, lb)

    def total(self, q, at):
        value = self.own[q, at]
        for side in ((0, 1) if q == 0 else (q - 1,)):
            value = value + self.into[side, at].astype(jnp.float32)
        return value

    def forward(self, chunk):
        for side in (0, 1):
            self.first[side, chunk].wait_recv()
        base = 4 * chunk
        spots = [(0, base), (0, base + 1), (1, base + 2), (1, base + 3), (2, base + 2), (2, base + 3)]
        for at, (q, spot) in enumerate(spots):
            self.out_far[chunk, at] = self.total(q, spot).astype(jnp.bfloat16)

    def start_far(self, chunk):
        db = 1 if chunk else -1
        src, dst = self.out_far.at[chunk], self.into_far.at[chunk]
        if self.out_mid is None:
            self.second[chunk] = self.wire(src, dst, self.places.home(0, db))
        else:
            self.second[chunk] = self.wire(src, dst, self.places.inward(db), self.places.apart(db))

    def settle(self):
        for side in (0, 1):
            self.first[side, 2].wait_recv()

    def start_middle(self):
        for at, (q, spot) in enumerate(self.MIDDLE):
            self.out_mid[at] = self.total(q, spot).astype(jnp.bfloat16)
        self.second[2] = self.wire(
            self.out_mid, self.into_mid, self.places.inward(0), self.places.apart(0)
        )

    def middle(self, q, spot):
        if self.out_mid is None:
            return self.total(q, spot)
        return self.into_mid[self.MIDDLE.index((q, spot))].astype(jnp.float32)

    def finish(self, emit):
        for copy in self.second.values():
            copy.wait_recv()

        def far(chunk, at):
            return self.into_far[chunk, at].astype(jnp.float32)

        emit(0, 0, self.middle(0, 8) + far(0, 0) + far(1, 0))
        emit(0, 1, self.middle(0, 5) + far(0, 1))
        emit(0, -1, (self.middle(0, 1) + far(1, 1)).T)
        for q, pa in ((1, self.outer), (2, -self.outer)):
            emit(pa, 0, self.middle(q, 10) + far(0, 2 * q) + far(1, 2 * q))
            emit(pa, 1, self.middle(q, 9) + far(0, 2 * q + 1))
            emit(pa, -1, self.middle(q, 11) + far(1, 2 * q + 1))


def prepare(orb, pot, lefts, rights):
    width, cells = orb.shape[-2], orb.shape[-1]
    lane = lax.broadcasted_iota(jnp.int32, (width, 128), 1)
    for ka in range(3):
        for kb in range(3):
            source = orb[ka, kb]
            value = source.astype(jnp.float32)
            lefts[ka, kb, :, :cells] = source
            rights[ka, kb, :, :cells] = (value * pot[0]).astype(jnp.bfloat16)
            for line in range(cells // 128):
                piece = value[:, line * 128:(line + 1) * 128]
                ahead = pltpu.roll(piece, 127, 1)
                step = jnp.where(lane < 127, ahead - piece, 0.0).astype(jnp.bfloat16)
                at = cells + line * 128
                rights[ka, kb, :, at:at + 128] = step
                lefts[ka, kb, :, at:at + 128] = (step.astype(jnp.float32) * 0.5).astype(jnp.bfloat16)


def kernel(counts, orb_in, pot_in, den_in, pattern, ham, mar, pur,
           v_near, d_near, f_near, g_near, m_near, u_near, lefts, rights,
           s_own, s_out, s_into, s_far, s_back, h_own, h_out, h_into, h_far, h_back,
           s_mid, s_core, v_base, d_base, u_base,
           u_col, t_col, d_col, d_row, o_col, o_row, orb, pot, den, ham_own, mar_own, pur_own, sums, load, send, recv):
    width = orb.shape[-2]
    places = Places(counts)

    def keep(pa, pb):
        return pattern[3 * (1 + pa) + 1 + pb].astype(jnp.float32)

    loads = [
        pltpu.make_async_copy(src, dst, load.at[at])
        for at, (src, dst) in enumerate(((orb_in, orb), (den_in, den), (pot_in, pot)))
    ]
    for copy in loads:
        copy.start()
    barrier = pltpu.get_barrier_semaphore()
    greeted = places.greet(barrier)

    wire = Wire(send, recv)
    s_sum = Gram(wire, places, orb, orb, s_own, s_out, s_into, s_far, s_back, s_mid, s_core)
    h_sum = Gram(wire, places, lefts, rights, h_own, h_out, h_into, h_far, h_back)
    fields = Halo(wire, places, v_near, v_base, whole=True)
    density = Halo(wire, places, d_near, d_base)
    firsts = Halo(wire, places, f_near, split=True)
    seconds = Halo(wire, places, g_near, split=True)
    margin = Slim(wire, places, u_near)

    loads[0].wait()
    s_sum.compute_sent(0)
    loads[1].wait()
    loads[2].wait()
    for pa in SPAN:
        for pb in SPAN:
            at = 3 * pa + pb + 4
            v_base[at:at + 1] = jnp.full((1, 128), keep(pa, pb), jnp.float32)
            block = den[pa + 1, pb + 1].astype(jnp.float32) * keep(pa, pb)
            d_base[pa + 1, pb + 1] = block.astype(jnp.bfloat16)
    pl.semaphore_wait(barrier, greeted)

    for chunk in (0, 1):
        s_sum.start(0, chunk)
    fields.start_far()
    density.start_far()
    s_sum.start(0, 2)
    s_sum.compute_sent(1)
    for chunk in (0, 1, 2):
        s_sum.start(1, chunk)
    s_sum.compute_own()
    prepare(orb, pot, lefts, rights)
    for side in (0, 1):
        h_sum.compute_sent(side)
    h_sum.compute_own()
    fields.relay()
    for chunk in (0, 1):
        s_sum.forward(chunk)
        s_sum.start_far(chunk)
    density.relay(0, 3)
    s_sum.settle()
    s_sum.start_middle()
    density.relay(3)
    for side in (0, 1):
        h_sum.start(side, 0)
    fields.finish()

    def mask(ja, jb, pa, pb):
        at = 3 * (1 + pa) + 1 + pb
        return v_near[1 + ja, 1 + jb, pl.ds(at, 1), :width]

    def put_margin(a, b, value):
        m_near[1, 1, 1 + a, 1 + b] = (value * mask(0, 0, a, b)).astype(jnp.bfloat16)
        u_near[1, 1, 1 + a, 1 + b] = value.astype(jnp.bfloat16)
        u_col[1 + a, 1 + b] = (value * mask(a, b, -a, -b)).astype(jnp.bfloat16)

    s_sum.finish(put_margin)
    density.finish()

    def put_first(a, b, value):
        f_near[1, 1, 1 + a, 1 + b] = (value * mask(a, b, -a, -b)).astype(jnp.bfloat16)

    rows = groups(places.outer)
    for at, (ka, fas) in enumerate(rows):
        give(width, ka, column(
            width,
            lambda k, f: d_near[1 + k[0], 1 + k[1], 1 + f[0] - k[0], 1 + f[1] - k[1]],
            lambda f: u_col[1 + f[0], 1 + f[1]],
            True, ka, fas,
        ), put_first)
        firsts.ready(at)
    firsts.relay(0, 2)
    firsts.cross()
    firsts.relay(2)
    margin.start_far()
    margin.start_near()
    h_sum.forward(0)
    h_sum.start_far(0)

    def complete(local):
        for ja, jb in AROUND:
            for ka in SPAN:
                for kb in SPAN:
                    pa, pb = ka - ja, kb - jb
                    if abs(pa) > 1 or abs(pb) > 1 or local != ((ka, kb) == (0, 0)):
                        continue
                    if not local and Slim.sent(ja, jb, pa, pb):
                        block = u_near[ja + 1, jb + 1, pa + 1, pb + 1].astype(jnp.float32)
                    else:
                        block = u_near[ka + 1, kb + 1, 1 - pa, 1 - pb].astype(jnp.float32).T
                    kept = block * mask(ja, jb, pa, pb)
                    m_near[ja + 1, jb + 1, pa + 1, pb + 1] = kept.astype(jnp.bfloat16)

    complete(True)

    def put_third(a, b, value):
        kept = value * mask(a, b, -a, -b)
        pur_own[1 + a, 1 + b] = 3.0 * kept
        t_col[1 + a, 1 + b] = kept.astype(jnp.bfloat16)

    def finish_step(lefts_at, out, send):
        for at, (ka, fas) in enumerate(rows):
            def put_fifth(a, b, value):
                kept = value * mask(a, b, -a, -b)
                out[1 + a, 1 + b] = (pur_own[1 + a, 1 + b] - 2.0 * kept).astype(jnp.bfloat16)

            give(width, ka, column(
                width, lefts_at, lambda f: t_col[1 + f[0], 1 + f[1]], False, ka, fas
            ), put_fifth)
            for kb in SPAN:
                send(at, ka, kb)

    def first_at(k, f):
        return f_near[1 + f[0], 1 + f[1], 1 + k[0] - f[0], 1 + k[1] - f[1]]

    def density_at(f):
        return d_near[1 + f[0], 1 + f[1], 1 - f[0], 1 - f[1]]

    firsts.finish_inner()
    outer = places.outer
    sums[0] = column(width, first_at, density_at, False, outer, (0,))
    sums[1] = column(width, first_at, density_at, False, 0, (0, -outer))
    give(width, -outer, column(width, first_at, density_at, False, -outer, (0, -outer)), put_third)
    firsts.finish_outer()
    for at, ka in enumerate((outer, 0)):
        give(width, ka, column(width, first_at, density_at, False, ka, (outer,), sums[at]), put_third)

    turned = []

    def send_turn(at, a, b):
        if at == 1 and b == 0:
            d_row[1, 1] = d_col[1, 1]
        else:
            turned.append(wire(d_col.at[1 + a, 1 + b], d_row.at[1 - a, 1 - b], places.near(a, b)))

    finish_step(first_at, d_col, send_turn)
    margin.relay()
    back = wire(u_near.at[1, 1], u_base, places.outward(0, 0), places.away(0))
    for side in (0, 1):
        h_sum.start(side, 1)
    margin.finish()
    complete(False)
    for copy in turned:
        copy.wait_recv()

    def put_second(a, b, value):
        g_near[1, 1, 1 + a, 1 + b] = (value * mask(0, 0, a, b)).astype(jnp.bfloat16)

    product(d_row, m_near, outer, put_second, seconds.ready)
    seconds.relay(0, 2)
    seconds.cross()
    seconds.relay(2)
    for side in (0, 1):
        h_sum.start(side, 2)
    h_sum.forward(1)
    h_sum.start_far(1)
    def second_at(k, f):
        return g_near[1 + k[0], 1 + k[1], 1 + f[0] - k[0], 1 + f[1] - k[1]]

    def purer_at(f):
        return d_col[1 + f[0], 1 + f[1]]

    seconds.finish_inner()
    for ka, fas in (rows[1], rows[2]):
        give(width, ka, column(width, second_at, purer_at, False, ka, fas), put_third)
    seconds.finish_outer()
    give(width, outer, column(width, second_at, purer_at, False, *rows[0]), put_third)
    turned_out = []

    def send_out(at, a, b):
        turned_out.append(wire(
            o_col.at[1 + a, 1 + b], o_row.at[1 - a, 1 - b], places.outward(a, b),
            places.away(b) if at == 1 else None,
        ))

    finish_step(second_at, o_col, send_out)

    def put_ham(a, b, value):
        ham_own[1 + a, 1 + b] = value * keep(a, b)

    h_sum.settle()
    h_sum.finish(put_ham)
    saves = [
        pltpu.make_async_copy(src, dst, load.at[3 + at])
        for at, (src, dst) in enumerate(((ham_own, ham), (mar_own, mar), (pur_own, pur)))
    ]
    saves[0].start()
    back.wait_recv()
    for a, b in AROUND + [(0, 0)]:
        mar_own[1 + a, 1 + b] = u_base[1 + a, 1 + b].astype(jnp.float32) * keep(a, b)
    saves[1].start()
    for copy in turned_out:
        copy.wait_recv()
    for a in range(3):
        for b in range(3):
            pur_own[a, b] = o_row[a, b].astype(jnp.float32)
    saves[2].start()
    wire.drain()
    for copy in saves:
        copy.wait()


def store(*refs):
    count = (len(refs) - 1) // 3
    loads, saves = (
        [
            pltpu.make_async_copy(src, dst, refs[-1].at[base + at])
            for at, (src, dst) in enumerate(zip(srcs, dsts))
        ]
        for base, srcs, dsts in (
            (0, refs[:count], refs[2 * count:-1]), (count, refs[2 * count:-1], refs[count:2 * count])
        )
    )
    for copy in loads:
        copy.start()
    for one, other in zip(loads, saves):
        one.wait()
        other.start()
    for copy in saves:
        copy.wait()


def body(counts, orbitals, potential, density, pattern):
    width, cells = orbitals.shape[3], orbitals.shape[4]
    low = jnp.bfloat16
    near = pltpu.VMEM((3, 3, 3, 3, width, width), low)
    some = pltpu.VMEM((3, 3, width, width), low)
    blocks = jax.ShapeDtypeStruct((3, 3, width, width), jnp.float32)
    vmem = pl.BlockSpec(memory_space=pltpu.VMEM)
    pairs = [
        pltpu.VMEM((3, 12, width, width), jnp.float32),
        pltpu.VMEM((2, 12, width, width), low),
        pltpu.VMEM((2, 12, width, width), low),
        pltpu.VMEM((2, 6, width, width), low),
        pltpu.VMEM((2, 6, width, width), low),
    ]
    outs = pl.pallas_call(
        functools.partial(kernel, counts),
        out_shape=(blocks,) * 3,
        in_specs=[pl.BlockSpec(memory_space=pl.ANY)] * 3 + [pl.BlockSpec(memory_space=pltpu.SMEM)],
        out_specs=(pl.BlockSpec(memory_space=pltpu.HBM),) * 3,
        scratch_shapes=[
            pltpu.VMEM((3, 3, 16, 128), jnp.float32),
            near, near, near, near, near,
            pltpu.VMEM((3, 3, width, 2 * cells), low),
            pltpu.VMEM((3, 3, width, 2 * cells), low),
            *pairs, *pairs,
            pltpu.VMEM((9, width, width), low),
            pltpu.VMEM((9, width, width), low),
            pltpu.VMEM((16, 128), jnp.float32),
            some, some,
            some, some, some, some, some, some,
            pltpu.VMEM((3, 3, width, cells), low),
            pltpu.VMEM((1, 1, cells), jnp.float32),
            some,
            *[pltpu.VMEM((3, 3, width, width), jnp.float32)] * 3,
            pltpu.VMEM((2, 3 * width, width), jnp.float32),
            pltpu.SemaphoreType.DMA((6,)),
            pltpu.SemaphoreType.DMA((PORTS,)),
            pltpu.SemaphoreType.DMA((PORTS,)),
        ],
        compiler_params=pltpu.CompilerParams(
            collective_id=0, has_side_effects=True, vmem_limit_bytes=60 * 2**20
        ),
    )(
        orbitals.reshape(3, 3, width, cells),
        potential.reshape(1, 1, cells),
        density.reshape(3, 3, width, width),
        pattern.reshape(9),
    )
    outs = pl.pallas_call(
        store,
        out_shape=(blocks,) * 3,
        in_specs=[pl.BlockSpec(memory_space=pl.ANY)] * 3,
        out_specs=[pl.BlockSpec(memory_space=pltpu.HBM)] * 3,
        scratch_shapes=[pltpu.VMEM((3, 3, width, width), jnp.float32)] * 3
        + [pltpu.SemaphoreType.DMA((6,))],
        compiler_params=pltpu.CompilerParams(vmem_limit_bytes=60 * 2**20),
    )(*outs)
    return tuple(out.reshape(1, 1, 9, width, width) for out in outs)


def solution(mesh):
    rows = P("gx", "yz", None, None, None)
    flat = P("gx", "yz", None)
    return jax.shard_map(
        functools.partial(body, (mesh.shape["gx"], mesh.shape["yz"])),
        mesh=mesh,
        in_specs=(rows, flat, rows, flat),
        out_specs=(rows,) * 3,
        check_vma=False,
    )
```

time: 99.7 us -> 74.4 us (0.75)
  the two profiles are of different devices: /device:TPU:1 before, /device:TPU:27 now
where the time goes in v1:
time: 74.4 us; the launch traced here: 74.2 us
  Pallas kernels  73.6 us (99%)
    pallas_call x1, Pallas kernels, body(): pl.pallas_call(functools.partial(kernel, counts), out_shape=(blocks,) * 3...  71.3 us
    pallas_call x1, Pallas kernels, body(): pl.pallas_call(store, out_shape=(blocks,) * 3, in_specs=[pl.BlockSpec(mem...  2.32 us

profile of v1, /device:TPU:27, one launch (start us, length us, event | category | flops | bytes accessed | tf_op | source)
XLA Modules:
  0.0 74.2 jit_solution(14673456615032917083)
XLA Ops:
  0.6 71.3 %shard_map.67 = (f32[3,3,128,128]{3,2,1,0:T(8,128)}, f32[3,3,128,128]{3,2,1,0:T(8,128)}, f32[3,3,128,128]{3,2,1,0:T(8,128)}) custom-call(bf16[3,3,128,256]{3,2,1,0:T(8,128)(2,1)} %bitcast.6, f32[1,1,256]{2,1,0:T(1,128)} %pot_in.1, bf16[3,3,128,128]{3,2,1,0:T(8,128)(2,1)} %bitcast.7, s32[9]{0:T(128)} %bitcast.8), custom_call_target="tpu_custom_call" | custom-call | tf_op jit(solution)/shard_map/pallas_call | solution.py:682
  71.9 2.3 %shard_map.68 = (f32[3,3,128,128]{3,2,1,0:T(8,128)}, f32[3,3,128,128]{3,2,1,0:T(8,128)}, f32[3,3,128,128]{3,2,1,0:T(8,128)}) custom-call(f32[3,3,128,128]{3,2,1,0:T(8,128)} %get-tuple-element.9.refs_0_, f32[3,3,128,128]{3,2,1,0:T(8,128)} %get-tuple-element.10.refs_1_, f32[3,3,128,128]{3,2,1,0:T(8,128)} %get-tuple-element.11.refs_2_), custom_call_target="tpu_custom_call" | custom-call | tf_op jit(solution)/shard_map/pallas_call | solution.py:716

commit v2 on v1

--- a/solution.py
+++ b/solution.py
@@ -272,7 +272,7 @@
 def product(left, near, outer, emit, done):
     width = left.shape[-1]
     blank = jnp.zeros((width, width), jnp.bfloat16)
-    for at, (pa, fas) in enumerate(groups(outer)):
+    for pa, fas in groups(outer):
         total = None
         for fa in fas:
             lhs = jnp.concatenate([left[fa + 1, fb + 1] for fb in SPAN], axis=1)
@@ -286,6 +286,7 @@
             total = term if total is None else total + term
         for pb in SPAN:
             emit(pa, pb, total[:, (pb + 1) * width:(pb + 2) * width])
+    for at in range(3):
         done(at)
 
 
@@ -506,18 +507,19 @@
         f_near[1, 1, 1 + a, 1 + b] = (value * mask(a, b, -a, -b)).astype(jnp.bfloat16)
 
     rows = groups(places.outer)
-    for at, (ka, fas) in enumerate(rows):
+    for ka, fas in rows:
         give(width, ka, column(
             width,
             lambda k, f: d_near[1 + k[0], 1 + k[1], 1 + f[0] - k[0], 1 + f[1] - k[1]],
             lambda f: u_col[1 + f[0], 1 + f[1]],
             True, ka, fas,
         ), put_first)
+    for at in range(3):
         firsts.ready(at)
     firsts.relay(0, 2)
     firsts.cross()
+    margin.start_far()
     firsts.relay(2)
-    margin.start_far()
     margin.start_near()
     h_sum.forward(0)
     h_sum.start_far(0)
@@ -544,14 +546,15 @@
         t_col[1 + a, 1 + b] = kept.astype(jnp.bfloat16)
 
     def finish_step(lefts_at, out, send):
-        for at, (ka, fas) in enumerate(rows):
-            def put_fifth(a, b, value):
-                kept = value * mask(a, b, -a, -b)
-                out[1 + a, 1 + b] = (pur_own[1 + a, 1 + b] - 2.0 * kept).astype(jnp.bfloat16)
-
+        def put_fifth(a, b, value):
+            kept = value * mask(a, b, -a, -b)
+            out[1 + a, 1 + b] = (pur_own[1 + a, 1 + b] - 2.0 * kept).astype(jnp.bfloat16)
+
+        for ka, fas in rows:
             give(width, ka, column(
                 width, lefts_at, lambda f: t_col[1 + f[0], 1 + f[1]], False, ka, fas
             ), put_fifth)
+        for at, (ka, _) in enumerate(rows):
             for kb in SPAN:
                 send(at, ka, kb)
 

time: 74.4 us -> 74.2 us (level)
  no operation moved by 1% of the time
where the time goes in v2:
time: 74.2 us; the launch traced here: 74 us
  Pallas kernels  73.4 us (99%)
    pallas_call x1, Pallas kernels, body(): pl.pallas_call(functools.partial(kernel, counts), out_shape=(blocks,) * 3...  71 us
    pallas_call x1, Pallas kernels, body(): pl.pallas_call(store, out_shape=(blocks,) * 3, in_specs=[pl.BlockSpec(mem...  2.32 us

profile of v2, /device:TPU:27, one launch (start us, length us, event | category | flops | bytes accessed | tf_op | source)
XLA Modules:
  0.0 74.0 jit_solution(3000651506866246780)
XLA Ops:
  0.6 71.0 %shard_map.67 = (f32[3,3,128,128]{3,2,1,0:T(8,128)}, f32[3,3,128,128]{3,2,1,0:T(8,128)}, f32[3,3,128,128]{3,2,1,0:T(8,128)}) custom-call(bf16[3,3,128,256]{3,2,1,0:T(8,128)(2,1)} %bitcast.6, f32[1,1,256]{2,1,0:T(1,128)} %pot_in.1, bf16[3,3,128,128]{3,2,1,0:T(8,128)(2,1)} %bitcast.7, s32[9]{0:T(128)} %bitcast.8), custom_call_target="tpu_custom_call" | custom-call | tf_op jit(solution)/shard_map/pallas_call | solution.py:685
  71.7 2.3 %shard_map.68 = (f32[3,3,128,128]{3,2,1,0:T(8,128)}, f32[3,3,128,128]{3,2,1,0:T(8,128)}, f32[3,3,128,128]{3,2,1,0:T(8,128)}) custom-call(f32[3,3,128,128]{3,2,1,0:T(8,128)} %get-tuple-element.9.refs_0_, f32[3,3,128,128]{3,2,1,0:T(8,128)} %get-tuple-element.10.refs_1_, f32[3,3,128,128]{3,2,1,0:T(8,128)} %get-tuple-element.11.refs_2_), custom_call_target="tpu_custom_call" | custom-call | tf_op jit(solution)/shard_map/pallas_call | solution.py:719
